TPU v7x, 256 devices: a whole 4x4x8 slice. The times are simulated.
256 devices in a mesh: dp: 8 (over x_lo, y), mp: 32 (over z, x_hi, core).
Axes of the slice: x: 4 (x_hi: 2, x_lo: 2; x = x_hi * 2 + x_lo), y: 4, z: 8, core: 2. Of those that a mesh axis runs over, the one named last changes fastest.
Arguments:
- tokens: bfloat16 [1024, 6144], P(('dp', 'mp')), may hold values from -6 to 6
- norm_gain: float32 [6144], replicated, may hold values from 0.5 to 1.5
- w_query: bfloat16 [6144, 4096], P('dp', 'mp'), as said below
- w_key: bfloat16 [6144, 4096], P('dp', 'mp'), as said below
- w_value: bfloat16 [6144, 4096], P('dp', 'mp'), may hold values from -0.078125 to 0.078125
- w_inner: bfloat16 [6144, 24576], P('dp', 'mp'), may hold values from -0.078125 to 0.078125
- bias_inner: float32 [24576], P('mp'), may hold values from -3 to 3
- w_attn_out: bfloat16 [4096, 6144], P('mp', 'dp'), may hold values from -0.09375 to 0.09375
- w_outer: bfloat16 [24576, 6144], P('mp', 'dp'), may hold values from -0.0390625 to 0.0390625
- temper: float32 [32], P('mp'), may hold values from 0.5 to 24
Outputs:
- result: bfloat16 [1024, 6144], P(('dp', 'mp'))
Inputs may be any that keep to these rules, and one draw needn't show every extreme that they name: `w_query`: entries of order 6144 ** -0.5. `w_key`: entries of order 6144 ** -0.5.
All inputs are finite; a program needn't handle non-finite values.
Results may differ from a plain program's by a relative error of at most 0.023.
Values may be sent and summed in bfloat16 or wider, within the bound.
A program may use at most 64 MiB of HBM per device.

v0:
```python
import math

import jax
import jax.numpy as jnp
from jax import lax
from jax.sharding import Mesh
from jax.sharding import PartitionSpec as P

HEAD = 128
MP = ("mp_0", "mp_1", "mp_2")
DP_MP = ("dp", "mp_0", "mp_1", "mp_2")


def copy_for_each(shard, axis):
    copies = jnp.broadcast_to(shard, (lax.axis_size(axis), *shard.shape))
    return lax.all_to_all(copies, axis, split_axis=0, concat_axis=0, tiled=True)


def laid_out(tiles, dim):
    shape = list(tiles.shape[1:])
    shape[dim] *= tiles.shape[0]
    return jnp.moveaxis(tiles, 0, dim).reshape(shape)


def gathered_copies(shard, axis, dim):
    tiles = copy_for_each(shard, axis)
    return laid_out(tiles, dim)


def in_blocks(shard, dim, devices):
    before, after = (shard.shape[:dim], shard.shape[dim + 1 :])
    return jnp.moveaxis(shard.reshape(*before, devices, -1, *after), dim, 0)


def summed_on_arrival(shard, axis, dim):
    tiles = in_blocks(shard, dim, lax.axis_size(axis))
    arrived = lax.all_to_all(tiles, axis, split_axis=0, concat_axis=0, tiled=True)
    return arrived.astype(jnp.float32).sum(axis=0)


def side_by_side(arrays, axis, dim, along):
    widths = [a.shape[along] for a in arrays]
    both = jnp.concatenate(arrays, axis=along)
    whole = lax.all_gather(both, axis, axis=dim, tiled=True)
    return tuple(jnp.split(whole, [sum(widths[:k]) for k in range(1, len(widths))], axis=along))


def sum_by_chip_2(shard, chips, core, dim):
    sizes = (lax.axis_size(chips), lax.axis_size(core))
    tiles = in_blocks(shard, dim, sizes[0] * sizes[1])
    inside = tiles.shape[1:]
    tiles = tiles.reshape(*sizes, *inside).swapaxes(0, 1).reshape(-1, *inside)
    tiles = lax.psum_scatter(tiles, core, scatter_dimension=0, tiled=True)
    return lax.psum_scatter(tiles, chips, scatter_dimension=0, tiled=True)[0]


def normalize(values):
    center = values - jnp.mean(values, axis=-1, keepdims=True)
    spread = jnp.mean(center * center, axis=-1, keepdims=True)
    return center * lax.rsqrt(spread + 1e-06)


def per_device(
    tokens, norm_gain, w_query, w_key, w_value, w_inner, bias_inner, w_attn_out, w_outer, temper
):
    local = tokens.astype(jnp.float32)
    normed = (normalize(local) * norm_gain).astype(jnp.bfloat16)
    image = gathered_copies(normed, MP, 0)
    count_rows = image.shape[0]
    width_head = w_query.shape[1]
    spread_rows = lax.all_to_all(image, "dp", split_axis=1, concat_axis=0, tiled=True)
    stacked = jnp.concatenate((w_query, w_key, w_value, w_inner), axis=1)
    projected = summed_on_arrival(
        jnp.dot(spread_rows, stacked, preferred_element_type=jnp.float32).astype(jnp.bfloat16),
        "dp",
        0,
    )
    query_sum = projected[:, :width_head]
    key_sum = projected[:, width_head : 2 * width_head]
    value_sum = projected[:, 2 * width_head : 3 * width_head]
    inner_sum = projected[:, 3 * width_head :]
    heads_dev = width_head // HEAD
    shape = (count_rows, heads_dev, HEAD)
    query_norm = normalize(
        query_sum.astype(jnp.bfloat16).astype(jnp.float32).reshape(shape)
    ).astype(jnp.bfloat16)
    key_norm = normalize(key_sum.astype(jnp.bfloat16).astype(jnp.float32).reshape(shape)).astype(
        jnp.bfloat16
    )
    values = value_sum.astype(jnp.bfloat16).reshape(shape)
    scale = temper / math.sqrt(HEAD)
    scores = jnp.einsum("qhc,khc->hqk", query_norm, key_norm, preferred_element_type=jnp.float32)
    scores = scores * scale[:, None, None]
    probs = jax.nn.softmax(scores, axis=-1).astype(jnp.bfloat16)
    mixed = jnp.einsum("hqk,khc->qhc", probs, values, preferred_element_type=jnp.float32)
    mixed = mixed.astype(jnp.bfloat16).reshape(count_rows, width_head)
    inner = inner_sum + bias_inner
    activ = jax.nn.gelu(inner, approximate=False).astype(jnp.bfloat16)
    attn_full, outer_full = side_by_side((w_attn_out, w_outer), "dp", 1, 0)
    total = sum_by_chip_2(
        (
            jnp.dot(mixed, attn_full, preferred_element_type=jnp.float32)
            + jnp.dot(activ, outer_full, preferred_element_type=jnp.float32)
        ).astype(jnp.bfloat16),
        ("mp_0", "mp_1"),
        "mp_2",
        0,
    ).astype(jnp.float32)
    return (local + total).astype(jnp.bfloat16)


def solution(mesh):
    finer = Mesh(mesh.devices.reshape(mesh.shape["dp"], 8, 2, 2), ("dp", "mp_0", "mp_1", "mp_2"))
    return jax.shard_map(
        per_device,
        mesh=finer,
        in_specs=(
            P(DP_MP, None),
            P(),
            P("dp", MP),
            P("dp", MP),
            P("dp", MP),
            P("dp", MP),
            P(MP),
            P(MP, "dp"),
            P(MP, "dp"),
            P(MP),
        ),
        out_specs=P(DP_MP, None),
        check_vma=False,
    )
```

profile of v0, /device:TPU:8, one launch (start us, length us, event | category | flops | bytes accessed | tf_op | source)
XLA Modules:
  0.0 410.7 jit_solution(5217342773899840325)
XLA Ops:
  6.5 0.0 copy-start
  6.5 0.0 copy-start.1
  6.5 0.0 all-gather.2.cloned.1.call-start
  6.5 2.5 pad_maximum_fusion
  9.0 0.0 all-gather.2.cloned.1.call-update
  9.0 0.0 copy-done
  9.0 0.2 convert_reduce_fusion.1
  9.2 0.2 fusion.56
  9.5 0.0 copy-done.1
  9.5 0.1 fusion.58
  9.6 0.7 broadcast_in_dim.2
  10.3 51.8 %all_to_all.29 = bf16[32,4,6144]{2,1,0:T(4,128)(2,1)S(1)} all-to-all(bf16[32,4,6144]{2,1,0:T(4,128)(2,1)S(1)} %broadcast_in_dim.2), channel_id=1, replica_groups=mesh['dp'=8,'mp_0'=8,'mp_1'=2,'mp_2'=2] {'mp_0','mp_1','mp_2'}, dimensions={0} | all-to-all | bytes 3145728 | tf_op jit(solution)/shard_map/all_to_all | solution.py:16
  62.1 1.2 all_to_all.21
  63.3 0.3 copy.17
  63.6 0.0 copy-start.2
  63.6 0.0 copy-start.3
  63.6 0.0 copy-start.4
  63.6 0.0 copy-start.5
  63.6 40.8 %all_to_all.30 = bf16[128,8,768]{2,0,1:T(8,128)(2,1)S(1)} all-to-all(bf16[128,8,768]{2,0,1:T(8,128)(2,1)S(1)} %copy.17), channel_id=1, replica_groups=mesh['dp'=8,'mp_0'=8,'mp_1'=2,'mp_2'=2] {'dp'}, dimensions={1} | all-to-all | bytes 3145728 | tf_op jit(solution)/shard_map/all_to_all | solution.py:71
  104.5 0.0 copy-done.2
  104.5 0.0 copy-done.3
  104.5 0.0 copy-done.4
  104.5 0.0 copy-done.5
  104.5 3.7 convolution_convert_fusion
  108.2 5.8 %all-to-all-start.2 = ((bf16[8,128,1152]{2,1,0:T(8,128)(2,1)}), bf16[8,128,1152]{2,1,0:T(8,128)(2,1)S(1)}, u32[]{:S(2)}, u32[]{:S(2)}) async-start(bf16[8,128,1152]{2,1,0:T(8,128)(2,1)} %bitcast.23), calls=%async_computation.2 | async-start | bytes 4718592 | tf_op jit(solution)/shard_map/all_to_all | solution.py:37
  113.9 0.0 all-reduce.5.cloned.1.call-start
  114.6 0.0 copy-start.6
  114.6 46.7 %all-to-all-done.2 = bf16[8,128,1152]{2,1,0:T(8,128)(2,1)S(1)} async-done(((bf16[8,128,1152]{2,1,0:T(8,128)(2,1)}), bf16[8,128,1152]{2,1,0:T(8,128)(2,1)S(1)}, u32[]{:S(2)}, u32[]{:S(2)}) %all-to-all-start.2) | async-done | bytes 2359328 | tf_op jit(solution)/shard_map/all_to_all | solution.py:37
  161.4 0.3 convert_reduce_fusion
  161.7 0.1 convert_reduce_fusion.3
  161.8 0.2 fusion.66
  162.0 0.3 fusion.114
  162.4 18.3 %all-gather.2.cloned.1.call-done = bf16[896,6144]{1,0:T(8,128)(2,1)} async-done(((bf16[896,768]{1,0:T(8,128)(2,1)}), bf16[896,6144]{1,0:T(8,128)(2,1)}) %all-gather.2.cloned.1.call-update) | async-done | bytes 11010064 | tf_op jit(solution)/shard_map/all_gather | solution.py:44
  180.6 0.0 copy-done.6
  180.6 7.6 %fusion = f32[128,6144]{1,0:T(8,128)} fusion(bf16[896,6144]{1,0:T(8,128)(2,1)} %all-gather.2.cloned.1.call-done, f32[128,1152]{1,0:T(8,128)S(1)} %convert_reduce_fusion, f32[768]{0:T(1024)S(1)} %copy-done.6), kind=kOutput, calls=%fused_computation | convolution fusion | flops 1214447616 | bytes 12980224 | tf_op jit(solution)/shard_map/dot_general | solution.py:103
  188.3 3.1 fusion.2
  191.4 0.6 reshape_reshape.3
  192.0 0.0 copy-start.8
  192.0 1.8 copy.18
  193.9 0.0 copy-start.7
  193.9 0.0 all-reduce.5.cloned.1.call-update
  193.9 0.0 all-reduce.7.cloned.1.call-start
  193.9 0.0 copy-done.8
  193.9 0.6 dynamic-slice
  195.2 42.8 %all-reduce.5.cloned.1.call-done = bf16[32,4,6144]{2,1,0:T(4,128)(2,1)} async-done(((bf16[32,4,6144]{2,1,0:T(4,128)(2,1)}), bf16[32,4,6144]{2,1,0:T(4,128)(2,1)}) %all-reduce.5.cloned.1.call-update) | async-done | bytes 1572880
  238.0 2.3 constant_dynamic-slice_fusion
  240.3 0.0 all-reduce.7.cloned.1.call-update
  240.4 0.0 copy-done.7
  240.4 0.7 dynamic-slice.2
  241.0 161.0 %all-reduce.7.cloned.1.call-done = bf16[16,4,6144]{2,1,0:T(4,128)(2,1)} async-done(((bf16[16,4,6144]{2,1,0:T(4,128)(2,1)}), bf16[16,4,6144]{2,1,0:T(4,128)(2,1)}) %all-reduce.7.cloned.1.call-update) | async-done | bytes 786448
  402.1 2.1 fusion.59
  (7 shorter events, 0.1 us)
Async XLA Ops:
  6.5 2.5 copy-start
  6.5 2.9 copy-start.1
  6.5 174.1 %all-gather.2.cloned.1.call-start = ((), (), s32[]{:S(2)}) async-start(), calls=%async_computation.3 | async-start | bytes 12386304 | tf_op jit(solution)/shard_map/all_gather | solution.py:44
  63.6 40.9 %copy-start.2 = (bf16[768,768]{1,0:T(8,128)(2,1)S(1)}, bf16[768,768]{1,0:T(8,128)(2,1)}, u32[]{:S(2)}) copy-start(bf16[768,768]{1,0:T(8,128)(2,1)} %param.15) | copy-start | bytes 3538948
  63.6 40.9 %copy-start.3 = (bf16[768,128]{1,0:T(8,128)(2,1)S(1)}, bf16[768,128]{1,0:T(8,128)(2,1)}, u32[]{:S(2)}) copy-start(bf16[768,128]{1,0:T(8,128)(2,1)} %param.14) | copy-start | bytes 589828
  63.6 40.9 %copy-start.4 = (bf16[768,128]{1,0:T(8,128)(2,1)S(1)}, bf16[768,128]{1,0:T(8,128)(2,1)}, u32[]{:S(2)}) copy-start(bf16[768,128]{1,0:T(8,128)(2,1)} %param.13) | copy-start | bytes 589828
  63.6 40.9 %copy-start.5 = (bf16[768,128]{1,0:T(8,128)(2,1)S(1)}, bf16[768,128]{1,0:T(8,128)(2,1)}, u32[]{:S(2)}) copy-start(bf16[768,128]{1,0:T(8,128)(2,1)} %param.12) | copy-start | bytes 589828
  108.2 53.2 %all-to-all-start.2 = ((bf16[8,128,1152]{2,1,0:T(8,128)(2,1)}), bf16[8,128,1152]{2,1,0:T(8,128)(2,1)S(1)}, u32[]{:S(2)}, u32[]{:S(2)}) async-start(bf16[8,128,1152]{2,1,0:T(8,128)(2,1)} %bitcast.23), calls=%async_computation.2 | async-start | bytes 4718592 | tf_op jit(solution)/shard_map/all_to_all | solution.py:37
  113.9 124.1 %all-reduce.5.cloned.1.call-start = ((), (), s32[]{:S(2)}) async-start(), calls=%async_computation.4 | async-start | bytes 3145728
  114.6 66.0 %copy-start.6 = (f32[768]{0:T(1024)S(1)}, f32[768]{0:T(1024)}, u32[]{:S(2)}) copy-start(f32[768]{0:T(1024)} %param.16) | copy-start | bytes 9220
  192.0 1.9 copy-start.8
  193.9 46.5 %copy-start.7 = (u32[256]{0:T(256)S(1)}, u32[256]{0:T(256)}, u32[]{:S(2)}) copy-start(u32[256]{0:T(256)} %constant.88) | copy-start | bytes 3076
  193.9 208.2 %all-reduce.7.cloned.1.call-start = ((), (), s32[]{:S(2)}) async-start(), calls=%async_computation.5 | async-start | bytes 1572864
Sparse Core Ops, SparseCore 0:
  9.2 171.4 all-gather.1
  194.0 43.9 all-reduce.4
  240.6 161.3 all-reduce.6
where the time goes:
time: 411 us
  waiting for transfers between devices  269 us (65%)
  blocking collectives  92.6 us (23%)
  matrix products  14.7 us (4%)
  between operations  14.6 us (4%)
  local copies, waits for them, and re-layouts  8.21 us (2%)
  starting transfers between devices  5.83 us (1%)
  other arithmetic  5.76 us (1%)
    unnamed x5, waiting for transfers between devices  204 us
    all_to_all x1, blocking collectives, copy_for_each(): return lax.all_to_all(copies, axis, split_axis=0, concat_axis=0, tiled=True)  51.8 us
    all_to_all x1, waiting for transfers between devices, summed_on_arrival(): lax.all_to_all(tiles, axis, split_axis=0, concat_axis=0, tiled=True)  46.7 us
    all_to_all x1, blocking collectives, per_device(): lax.all_to_all(image, 'dp', split_axis=1, concat_axis=0, tiled=True)  40.8 us
    all_gather x1, waiting for transfers between devices, side_by_side(): whole = lax.all_gather(both, axis, axis=dim, tiled=True)  18.3 us
  transfers between devices with their start and end apart: 4, of which 4 were waited for; matrix products, arithmetic and copies ran while one was open for 2% of the time, Pallas kernels for 0%

commit v1 on v0

v1 whole, which is shorter than its diff:
```python
import math

import jax
import jax.numpy as jnp
from jax import lax
from jax.experimental import pallas as pl
from jax.experimental.pallas import tpu as pltpu
from jax.sharding import PartitionSpec as P

BF = jnp.bfloat16
F32 = jnp.float32
MESH = pl.DeviceIdType.MESH
HEAD = 128
BLK = 768
ROT = ((2, 1, 0), (1, 0, 2), (0, 2, 1))
CHUNKS = ((0, 1), (1, 3), (3, 5), (5, 7), (7, 8))
GCOLS = ((0, 384), (384, 640), (640, 896))


def first_unit(part, r):
    a, b, c = ROT[part]
    return ((r >> a) & 1) * 4 + ((r >> b) & 1) * 2 + ((r >> c) & 1)


def last_unit(part, r):
    a, b, c = ROT[part]
    return ((r >> a) & 1) + ((r >> b) & 1) * 2 + ((r >> c) & 1) * 4


def normalize(values):
    center = values - jnp.mean(values, axis=-1, keepdims=True)
    spread = jnp.mean(center * center, axis=-1, keepdims=True)
    return center * lax.rsqrt(spread + 1e-06)


def kernel(
    tok_ref, gain_ref, wq_ref, wk_ref, wv_ref, wi_ref, bias_ref, wa_ref, wo_ref, temper_ref,
    out_ref,
    w1, w2, nb, ga, xb,
    s1, r1, k1, s2, r2, k2, s3, r3, k3, yb,
    g0, g1, g2, xa, tb, d2s, d2r, zs, zr, fb, fr,
    wsem, pa_send, pa_recv, zg_send, zg_recv, dg_send, dg_recv,
    rs_send, rs_recv, ag_send, ag_recv, dr_send, dr_recv, zr_send, zr_recv, pf_send, pf_recv,
):
    dp = lax.axis_index("dp")
    mp = lax.axis_index("mp")
    xl, y = dp // 4, dp % 4
    z, q, core = mp // 4, mp % 4, mp % 2

    def near(r):
        ys = (y, y + 1 - 2 * (y % 2), 3 - y, (y + 2) % 4)[r % 4]
        return (1 - xl if r >= 4 else xl) * 4 + ys

    peers = [near(r) for r in range(8)]
    up = (z + 1 - 2 * core + 8) % 8
    down = (z - 1 + 2 * core + 8) % 8
    dev_up = (dp, up * 4 + q)
    dev_down = (dp, down * 4 + q)
    dev_pair = (dp, mp + 1 - 2 * core)
    half = pl.multiple_of(core * 64, 64)
    other = pl.multiple_of(64 - core * 64, 64)

    def send(src, dst, ssem, rsem, dev):
        pltpu.make_async_remote_copy(
            src_ref=src, dst_ref=dst, send_sem=ssem, recv_sem=rsem, device_id=dev, device_id_type=MESH
        ).start()

    def wait(ref, sem):
        pltpu.make_async_copy(ref, ref, sem).wait()

    loads = [
        pltpu.make_async_copy(wq_ref, w1.at[:, 0:128], wsem.at[0]),
        pltpu.make_async_copy(wk_ref, w1.at[:, 128:256], wsem.at[1]),
        pltpu.make_async_copy(wv_ref, w1.at[:, 256:384], wsem.at[2]),
        pltpu.make_async_copy(wi_ref, w1.at[:, 384:1152], wsem.at[3]),
        pltpu.make_async_copy(wa_ref, w2.at[0:128], wsem.at[4]),
        pltpu.make_async_copy(wo_ref, w2.at[128:896], wsem.at[5]),
    ]
    for load in loads:
        load.start()

    plane = [(r, s) for r in range(8) for s in range(4) if (r, s) != (0, 0)]
    plane_dev = {(r, s): (peers[r], z * 4 + (q + s) % 4) for r, s in plane}

    barrier = pltpu.get_barrier_semaphore()
    for key in plane:
        pl.semaphore_signal(barrier, inc=1, device_id=plane_dev[key], device_id_type=MESH)
    for dev in (dev_up, dev_down):
        pl.semaphore_signal(barrier, inc=1, device_id=dev, device_id_type=MESH)

    local = tok_ref[...].astype(F32)
    normed = (normalize(local) * gain_ref[...]).astype(BF)
    for j in range(8):
        nb[j] = normed[:, j * BLK : (j + 1) * BLK]
    pl.semaphore_wait(barrier, 33)

    for r, s in plane:
        send(nb.at[peers[r]], ga.at[r * 4 + q], pa_send, pa_recv, plane_dev[r, s])
    ga[q] = nb[dp]
    wait(ga.at[0:31], pa_recv)

    for r in range(8):
        unit = jnp.concatenate([ga[r * 4 + s].astype(F32) for s in range(4)], axis=0)
        xb[0, r * 16 : (r + 1) * 16, :] = unit.astype(BF)

    def ring_out(slot, to, h):
        rows = pl.ds(h * 64, 64)
        send(xb.at[slot, rows], xb.at[to, rows], zg_send, zg_recv.at[to // 2 * 2 + h], dev_up)

    for h in range(2):
        ring_out(0, 1, h)

    def ring_step(step):
        if step < 4:
            slot = 2 * step - 1
            for h in range(2):
                rows = pl.ds(h * 64, 64)
                wait(xb.at[slot, rows], zg_recv.at[slot // 2 * 2 + h])
                if step < 3:
                    ring_out(slot, slot + 2, h)
                send(xb.at[slot, rows], xb.at[slot + 1, rows], dg_send, dg_recv.at[slot // 2 * 2 + h], dev_pair)
            if step == 3:
                rows = pl.ds(half, 64)
                send(xb.at[slot, rows], xb.at[7, rows], zg_send, zg_recv.at[6], dev_up)
        else:
            rows = pl.ds(half, 64)
            wait(xb.at[7, rows], zg_recv.at[6])
            send(xb.at[7, rows], xb.at[7, rows], dg_send, dg_recv.at[6], dev_pair)

    def pair_step(step):
        if step < 4:
            slot = 2 * step
            for h in range(2):
                rows = pl.ds(h * 64, 64)
                wait(xb.at[slot, rows], dg_recv.at[(slot - 1) // 2 * 2 + h])
        else:
            wait(xb.at[7, pl.ds(other, 64)], dg_recv.at[6])

    cube = [tuple(peers[1 << d] for d in ROT[p]) for p in range(3)]

    def project(c):
        lo, hi = CHUNKS[c]
        rows = (hi - lo) * 128
        left = xb[lo:hi].reshape(rows, BLK)
        for p in range(3):
            res = jnp.dot(left, w1[:, p * 384 : (p + 1) * 384], preferred_element_type=F32)
            for k in range(lo, hi):
                for r in range(8):
                    at = (k - lo) * 128 + r * 16
                    u = first_unit(p, r)
                    if u >= 4:
                        s1[p, k, u - 4] = res[at : at + 16].astype(BF)
                    else:
                        k1[p, k, u] = res[at : at + 16]
            send(s1.at[p, lo:hi], r1.at[p, lo:hi], rs_send.at[0], rs_recv.at[c, p, 0], (cube[p][0], mp))

    def halve_1(c):
        lo, hi = CHUNKS[c]
        for p in range(3):
            wait(r1.at[p, lo:hi], rs_recv.at[c, p, 0])
            s2[p, lo:hi] = (k1[p, lo:hi, 2:4] + r1[p, lo:hi, 2:4].astype(F32)).astype(BF)
            send(s2.at[p, lo:hi], r2.at[p, lo:hi], rs_send.at[1], rs_recv.at[c, p, 1], (cube[p][1], mp))
            k2[p, lo:hi] = k1[p, lo:hi, 0:2] + r1[p, lo:hi, 0:2].astype(F32)

    def halve_2(c):
        lo, hi = CHUNKS[c]
        for p in range(3):
            wait(r2.at[p, lo:hi], rs_recv.at[c, p, 1])
            s3[p, lo:hi] = (k2[p, lo:hi, 1] + r2[p, lo:hi, 1].astype(F32)).astype(BF)
            send(s3.at[p, lo:hi], r3.at[p, lo:hi], rs_send.at[2], rs_recv.at[c, p, 2], (cube[p][2], mp))
            k3[p, lo:hi] = k2[p, lo:hi, 0] + r2[p, lo:hi, 0].astype(F32)

    def halve_3(c):
        lo, hi = CHUNKS[c]
        for p in range(3):
            wait(r3.at[p, lo:hi], rs_recv.at[c, p, 2])
            yb[p, lo:hi] = k3[p, lo:hi] + r3[p, lo:hi].astype(F32)

    for load in loads[:4]:
        load.wait()
    for t in range(8):
        if 1 <= t < 5:
            ring_step(t)
        if 0 <= t - 1 < 5:
            halve_1(t - 1)
        if 0 <= t - 2 < 5:
            halve_2(t - 2)
        if 0 <= t - 3 < 5:
            halve_3(t - 3)
        if t < 5:
            if t:
                pair_step(t)
            project(t)

    def put(ref, lo, hi, value):
        for k in range(8):
            ref[k, 0, :, lo:hi] = value[k * 16 : (k + 1) * 16]

    def activation(p, lo, hi):
        inner = yb[p].reshape(128, 384)[:, lo:hi] + bias_ref[:, (p - 1) * 384 + lo : (p - 1) * 384 + hi]
        return (0.5 * inner * (1.0 + lax.erf(inner * math.sqrt(0.5)))).astype(BF)

    put(g0, 128, 384, activation(1, 0, 256))
    put(g1, 0, 128, activation(1, 256, 384))
    put(g1, 128, 256, activation(2, 0, 128))
    put(g2, 0, 256, activation(2, 128, 384))

    heads = yb[0].reshape(128, 384)
    query = normalize(heads[:, 0:128].astype(BF).astype(F32)).astype(BF)
    keys = normalize(heads[:, 128:256].astype(BF).astype(F32)).astype(BF)
    values = heads[:, 256:384].astype(BF)
    scores = lax.dot_general(query, keys, (((1,), (1,)), ((), ())), preferred_element_type=F32)
    scores = scores * (temper_ref[...] / math.sqrt(HEAD))
    scores = jnp.exp(scores - jnp.max(scores, axis=-1, keepdims=True))
    probs = (scores / jnp.sum(scores, axis=-1, keepdims=True)).astype(BF)
    mixed = jnp.dot(probs, values, preferred_element_type=F32).astype(BF)
    put(g0, 0, 128, mixed)

    gs = (g0, g1, g2)
    back = CHUNKS[::-1]

    def double(c, stage):
        lo, hi = back[c]
        n = 1 << stage
        for p in range(3):
            if stage:
                m = n // 2
                wait(gs[p].at[lo:hi, m:n], ag_recv.at[c, p, stage - 1])
            send(
                gs[p].at[lo:hi, 0:n], gs[p].at[lo:hi, n : 2 * n],
                ag_send.at[p], ag_recv.at[c, p, stage], (cube[p][stage], mp),
            )

    def combine(c):
        lo, hi = back[c]
        for p in range(3):
            wait(gs[p].at[lo:hi, 4:8], ag_recv.at[c, p, 2])
            c0, c1 = GCOLS[p]
            for k in range(lo, hi):
                for r in range(8):
                    xa[k, r * 16 : (r + 1) * 16, c0:c1] = gs[p][k, last_unit(p, r)]
        left = xa[lo:hi].reshape((hi - lo) * 128, 896)
        for n in range(2):
            res = jnp.dot(left, w2[:, n * 384 : (n + 1) * 384], preferred_element_type=F32)
            tb[lo:hi, :, n * 384 : (n + 1) * 384] = res.reshape(hi - lo, 128, 384)
        if c == 0:
            d2s[3, 0:64] = tb[7, pl.ds(other, 64)].astype(BF)
            send(d2s.at[3, 0:64], d2r.at[3, 0:64], dr_send, dr_recv.at[3], dev_pair)
        elif c < 4:
            s = 4 - c
            d2s[s - 1] = tb[hi - 1].astype(BF)
            send(d2s.at[s - 1], d2r.at[s - 1], dr_send, dr_recv.at[s - 1], dev_pair)

    def ring_sum(c):
        if c == 0:
            wait(d2r.at[3, 0:64], dr_recv.at[3])
            zs[3, 0:64] = (tb[7, pl.ds(half, 64)] + d2r[3, 0:64].astype(F32)).astype(BF)
            send(zs.at[3, 0:64], zr.at[3, 0:64], zr_send, zr_recv.at[6], dev_down)
        elif c < 4:
            s = 4 - c
            lo, _ = back[c]
            wait(d2r.at[s - 1], dr_recv.at[s - 1])
            if c == 1:
                tb[lo] = tb[lo] + d2r[s - 1].astype(F32)
                wait(zr.at[3, 0:64], zr_recv.at[6])
                tb[lo, pl.ds(half, 64)] = tb[lo, pl.ds(half, 64)] + zr[3, 0:64].astype(F32)
            for h in range(2):
                rows = slice(h * 64, h * 64 + 64)
                part = tb[lo, rows]
                if c > 1:
                    wait(zr.at[s, rows], zr_recv.at[s * 2 + h])
                    part = part + d2r[s - 1, rows].astype(F32) + zr[s, rows].astype(F32)
                zs[s - 1, rows] = part.astype(BF)
                send(zs.at[s - 1, rows], zr.at[s - 1, rows], zr_send, zr_recv.at[(s - 1) * 2 + h], dev_down)
        else:
            for h in range(2):
                rows = slice(h * 64, h * 64 + 64)
                wait(zr.at[0, rows], zr_recv.at[h])
                part = tb[0, rows] + zr[0, rows].astype(F32)
                for r in range(4 * h, 4 * h + 4):
                    for s in range(4):
                        at = (r - 4 * h) * 16 + s * 4
                        fb[r * 4 + s] = part[at : at + 4].astype(BF)
                for r, s in plane:
                    if r // 4 == h:
                        send(
                            fb.at[r * 4 + (q + s) % 4], fr.at[r * 4 + q], pf_send, pf_recv, plane_dev[r, s]
                        )

    for t in range(8):
        if t < 5:
            double(t, 0)
        if 0 <= t - 1 < 5:
            double(t - 1, 1)
        if 0 <= t - 2 < 5:
            double(t - 2, 2)
        if 0 <= t - 3 < 5:
            if t == 3:
                for load in loads[4:]:
                    load.wait()
            combine(t - 3)
            ring_sum(t - 3)

    fr[q] = fb[q]
    wait(fr.at[0:31], pf_recv)
    for r in range(8):
        total = fr[r * 4].astype(F32)
        for s in range(1, 4):
            total = total + fr[r * 4 + s].astype(F32)
        cols = pl.ds(pl.multiple_of(peers[r] * BLK, BLK), BLK)
        out_ref[:, cols] = (tok_ref[:, cols].astype(F32) + total).astype(BF)

    wait(ga.at[0:31], pa_send)
    wait(xb.at[0:7, 0:64], zg_send)
    wait(xb.at[0:7, 0:64], dg_send)
    wait(s1, rs_send.at[0])
    wait(s2, rs_send.at[1])
    wait(s3, rs_send.at[2])
    for p in range(3):
        wait(gs[p].at[:, 0:7], ag_send.at[p])
    wait(d2s.at[:, 0:112], dr_send)
    wait(zs.at[:, 0:112], zr_send)
    wait(fb.at[0:31], pf_send)


def per_device(tokens, gain, w_query, w_key, w_value, w_inner, bias, w_attn_out, w_outer, temper):
    vmem = pl.BlockSpec(memory_space=pltpu.VMEM)
    anyw = pl.BlockSpec(memory_space=pl.ANY)
    dma = pltpu.SemaphoreType.DMA
    return pl.pallas_call(
        kernel,
        out_shape=jax.ShapeDtypeStruct(tokens.shape, BF),
        in_specs=[vmem, vmem, anyw, anyw, anyw, anyw, vmem, anyw, anyw, vmem],
        out_specs=vmem,
        scratch_shapes=[
            pltpu.VMEM((768, 1152), BF),
            pltpu.VMEM((896, 768), BF),
            pltpu.VMEM((8, 4, BLK), BF),
            pltpu.VMEM((32, 4, BLK), BF),
            pltpu.VMEM((8, 128, BLK), BF),
            pltpu.VMEM((3, 8, 4, 16, 384), BF),
            pltpu.VMEM((3, 8, 4, 16, 384), BF),
            pltpu.VMEM((3, 8, 4, 16, 384), F32),
            pltpu.VMEM((3, 8, 2, 16, 384), BF),
            pltpu.VMEM((3, 8, 2, 16, 384), BF),
            pltpu.VMEM((3, 8, 2, 16, 384), F32),
            pltpu.VMEM((3, 8, 16, 384), BF),
            pltpu.VMEM((3, 8, 16, 384), BF),
            pltpu.VMEM((3, 8, 16, 384), F32),
            pltpu.VMEM((3, 8, 16, 384), F32),
            pltpu.VMEM((8, 8, 16, 384), BF),
            pltpu.VMEM((8, 8, 16, 256), BF),
            pltpu.VMEM((8, 8, 16, 256), BF),
            pltpu.VMEM((8, 128, 896), BF),
            pltpu.VMEM((8, 128, BLK), F32),
            pltpu.VMEM((4, 128, BLK), BF),
            pltpu.VMEM((4, 128, BLK), BF),
            pltpu.VMEM((4, 128, BLK), BF),
            pltpu.VMEM((4, 128, BLK), BF),
            pltpu.VMEM((32, 4, BLK), BF),
            pltpu.VMEM((32, 4, BLK), BF),
            dma((6,)),
            dma, dma,
            dma, dma((7,)),
            dma, dma((7,)),
            dma((3,)), dma((5, 3, 3)),
            dma((3,)), dma((5, 3, 3)),
            dma, dma((4,)),
            dma, dma((7,)),
            dma, dma,
        ],
        compiler_params=pltpu.CompilerParams(
            collective_id=0, has_side_effects=True, vmem_limit_bytes=60 * 1024 * 1024
        ),
    )(
        tokens, gain.reshape(1, -1), w_query, w_key, w_value, w_inner, bias.reshape(1, -1),
        w_attn_out, w_outer, temper.reshape(1, 1),
    )


def solution(mesh):
    return jax.shard_map(
        per_device,
        mesh=mesh,
        in_specs=(
            P(("dp", "mp"), None),
            P(),
            P("dp", "mp"),
            P("dp", "mp"),
            P("dp", "mp"),
            P("dp", "mp"),
            P("mp"),
            P("mp", "dp"),
            P("mp", "dp"),
            P("mp"),
        ),
        out_specs=P(("dp", "mp"), None),
        check_vma=False,
    )
```

time: 411 us -> 87.4 us (0.21)
  the two profiles are of different devices: /device:TPU:8 before, /device:TPU:1 now
where the time goes in v1:
time: 87.4 us; the launch traced here: 87.2 us
  Pallas kernels  83.9 us (96%)
  local copies, waits for them, and re-layouts  2.7 us (3%)
    pallas_call x1, Pallas kernels, per_device(): pl.pallas_call(kernel, out_shape=jax.ShapeDtypeStruct(tokens.shape, BF),...  83.9 us

profile of v1, /device:TPU:1, one launch (start us, length us, event | category | flops | bytes accessed | tf_op | source)
XLA Modules:
  0.0 87.2 jit_solution(5660937539887561097)
XLA Ops:
  0.7 1.3 %reshape.10.bias_ref = f32[1,768]{1,0:T(1,128)} reshape(f32[768]{0:T(1024)} %param.16) | data formatting | bytes 6144 | tf_op jit(solution)/shard_map/reshape | solution.py:376
  1.9 83.9 %shard_map.100 = bf16[4,6144]{1,0:T(4,128)(2,1)} custom-call(bf16[4,6144]{1,0:T(4,128)(2,1)} %tok_ref.1, f32[1,6144]{1,0:T(1,128)} %bitcast.3, bf16[768,128]{1,0:T(8,128)(2,1)} %wq_ref.1, bf16[768,128]{1,0:T(8,128)(2,1)} %wk_ref.1, bf16[768,128]{1,0:T(8,128)(2,1)} %wv_ref.1, bf16[768,768]{1,0:T(8,128)(2,1)} %wi_ref.1, f32[1,768]{1,0:T(1,128)} %reshape.10.bias_ref, ...), custom_call_target="tpu_custom_call" | custom-call | tf_op jit(solution)/shard_map/pallas_call | solution.py:330
  85.8 1.4 %copy.13 = bf16[4,6144]{1,0:T(4,128)(2,1)} copy(bf16[4,6144]{1,0:T(4,128)(2,1)} %shard_map.100) | data formatting | bytes 98304

commit v2 on v1

--- a/solution.py
+++ b/solution.py
@@ -88,20 +88,24 @@
     for dev in (dev_up, dev_down):
         pl.semaphore_signal(barrier, inc=1, device_id=dev, device_id_type=MESH)
 
-    local = tok_ref[...].astype(F32)
-    normed = (normalize(local) * gain_ref[...]).astype(BF)
-    for j in range(8):
-        nb[j] = normed[:, j * BLK : (j + 1) * BLK]
-    pl.semaphore_wait(barrier, 33)
-
-    for r, s in plane:
-        send(nb.at[peers[r]], ga.at[r * 4 + q], pa_send, pa_recv, plane_dev[r, s])
-    ga[q] = nb[dp]
-    wait(ga.at[0:31], pa_recv)
-
-    for r in range(8):
-        unit = jnp.concatenate([ga[r * 4 + s].astype(F32) for s in range(4)], axis=0)
-        xb[0, r * 16 : (r + 1) * 16, :] = unit.astype(BF)
+    def exchange():
+        local = tok_ref[...].astype(F32)
+        normed = (normalize(local) * gain_ref[...]).astype(BF)
+        for j in range(8):
+            nb[j] = normed[:, j * BLK : (j + 1) * BLK]
+        with jax.named_scope('barrier'):
+            pl.semaphore_wait(barrier, 33)
+
+        for r, s in plane:
+            send(nb.at[peers[r]], ga.at[r * 4 + q], pa_send, pa_recv, plane_dev[r, s])
+        ga[q] = nb[dp]
+        wait(ga.at[0:31], pa_recv)
+
+        for r in range(8):
+            unit = jnp.concatenate([ga[r * 4 + s].astype(F32) for s in range(4)], axis=0)
+            xb[0, r * 16 : (r + 1) * 16, :] = unit.astype(BF)
+
+    exchange()
 
     def ring_out(slot, to, h):
         rows = pl.ds(h * 64, 64)
@@ -181,40 +185,43 @@
     for t in range(8):
         if 1 <= t < 5:
             ring_step(t)
+            pair_step(t)
+        if t < 5:
+            project(t)
         if 0 <= t - 1 < 5:
             halve_1(t - 1)
         if 0 <= t - 2 < 5:
             halve_2(t - 2)
         if 0 <= t - 3 < 5:
             halve_3(t - 3)
-        if t < 5:
-            if t:
-                pair_step(t)
-            project(t)
-
-    def put(ref, lo, hi, value):
-        for k in range(8):
-            ref[k, 0, :, lo:hi] = value[k * 16 : (k + 1) * 16]
-
-    def activation(p, lo, hi):
-        inner = yb[p].reshape(128, 384)[:, lo:hi] + bias_ref[:, (p - 1) * 384 + lo : (p - 1) * 384 + hi]
-        return (0.5 * inner * (1.0 + lax.erf(inner * math.sqrt(0.5)))).astype(BF)
-
-    put(g0, 128, 384, activation(1, 0, 256))
-    put(g1, 0, 128, activation(1, 256, 384))
-    put(g1, 128, 256, activation(2, 0, 128))
-    put(g2, 0, 256, activation(2, 128, 384))
-
-    heads = yb[0].reshape(128, 384)
-    query = normalize(heads[:, 0:128].astype(BF).astype(F32)).astype(BF)
-    keys = normalize(heads[:, 128:256].astype(BF).astype(F32)).astype(BF)
-    values = heads[:, 256:384].astype(BF)
-    scores = lax.dot_general(query, keys, (((1,), (1,)), ((), ())), preferred_element_type=F32)
-    scores = scores * (temper_ref[...] / math.sqrt(HEAD))
-    scores = jnp.exp(scores - jnp.max(scores, axis=-1, keepdims=True))
-    probs = (scores / jnp.sum(scores, axis=-1, keepdims=True)).astype(BF)
-    mixed = jnp.dot(probs, values, preferred_element_type=F32).astype(BF)
-    put(g0, 0, 128, mixed)
+
+    def attend():
+        def put(ref, lo, hi, value):
+            for k in range(8):
+                ref[k, 0, :, lo:hi] = value[k * 16 : (k + 1) * 16]
+
+        def activation(p, lo, hi):
+            inner = yb[p].reshape(128, 384)[:, lo:hi] + bias_ref[(p - 1) * 384 + lo : (p - 1) * 384 + hi].reshape(1, hi - lo)
+            return (0.5 * inner * (1.0 + lax.erf(inner * math.sqrt(0.5)))).astype(BF)
+
+        put(g0, 128, 384, activation(1, 0, 256))
+        put(g1, 0, 128, activation(1, 256, 384))
+        put(g1, 128, 256, activation(2, 0, 128))
+        put(g2, 0, 256, activation(2, 128, 384))
+
+        heads = yb[0].reshape(128, 384)
+        query = normalize(heads[:, 0:128].astype(BF).astype(F32)).astype(BF)
+        keys = normalize(heads[:, 128:256].astype(BF).astype(F32)).astype(BF)
+        values = heads[:, 256:384].astype(BF)
+        scores = lax.dot_general(query, keys, (((1,), (1,)), ((), ())), preferred_element_type=F32)
+        scores = scores * (temper_ref[...] / math.sqrt(HEAD))
+        scores = jnp.exp(scores - jnp.max(scores, axis=-1, keepdims=True))
+        probs = (scores / jnp.sum(scores, axis=-1, keepdims=True)).astype(BF)
+        mixed = jnp.dot(probs, values, preferred_element_type=F32).astype(BF)
+        put(g0, 0, 128, mixed)
+
+
+    attend()
 
     gs = (g0, g1, g2)
     back = CHUNKS[::-1]
@@ -287,40 +294,47 @@
                             fb.at[r * 4 + (q + s) % 4], fr.at[r * 4 + q], pf_send, pf_recv, plane_dev[r, s]
                         )
 
-    for t in range(8):
+    for t in range(5):
+        double(t, 0)
+    for t in range(7):
         if t < 5:
-            double(t, 0)
+            double(t, 1)
         if 0 <= t - 1 < 5:
-            double(t - 1, 1)
+            double(t - 1, 2)
         if 0 <= t - 2 < 5:
-            double(t - 2, 2)
-        if 0 <= t - 3 < 5:
-            if t == 3:
+            if t == 2:
                 for load in loads[4:]:
                     load.wait()
-            combine(t - 3)
-            ring_sum(t - 3)
-
-    fr[q] = fb[q]
-    wait(fr.at[0:31], pf_recv)
-    for r in range(8):
-        total = fr[r * 4].astype(F32)
-        for s in range(1, 4):
-            total = total + fr[r * 4 + s].astype(F32)
-        cols = pl.ds(pl.multiple_of(peers[r] * BLK, BLK), BLK)
-        out_ref[:, cols] = (tok_ref[:, cols].astype(F32) + total).astype(BF)
-
-    wait(ga.at[0:31], pa_send)
-    wait(xb.at[0:7, 0:64], zg_send)
-    wait(xb.at[0:7, 0:64], dg_send)
-    wait(s1, rs_send.at[0])
-    wait(s2, rs_send.at[1])
-    wait(s3, rs_send.at[2])
-    for p in range(3):
-        wait(gs[p].at[:, 0:7], ag_send.at[p])
-    wait(d2s.at[:, 0:112], dr_send)
-    wait(zs.at[:, 0:112], zr_send)
-    wait(fb.at[0:31], pf_send)
+            combine(t - 2)
+            ring_sum(t - 2)
+
+    def finish():
+        fr[q] = fb[q]
+        wait(fr.at[0:31], pf_recv)
+        for r in range(8):
+            total = fr[r * 4].astype(F32)
+            for s in range(1, 4):
+                total = total + fr[r * 4 + s].astype(F32)
+            cols = pl.ds(pl.multiple_of(peers[r] * BLK, BLK), BLK)
+            out_ref[:, cols] = (tok_ref[:, cols].astype(F32) + total).astype(BF)
+
+
+    finish()
+
+    def drain():
+        wait(ga.at[0:31], pa_send)
+        wait(xb.at[0:7, 0:64], zg_send)
+        wait(xb.at[0:7, 0:64], dg_send)
+        wait(s1, rs_send.at[0])
+        wait(s2, rs_send.at[1])
+        wait(s3, rs_send.at[2])
+        for p in range(3):
+            wait(gs[p].at[:, 0:7], ag_send.at[p])
+        wait(d2s.at[:, 0:112], dr_send)
+        wait(zs.at[:, 0:112], zr_send)
+        wait(fb.at[0:31], pf_send)
+
+    drain()
 
 
 def per_device(tokens, gain, w_query, w_key, w_value, w_inner, bias, w_attn_out, w_outer, temper):
@@ -373,7 +387,7 @@
             collective_id=0, has_side_effects=True, vmem_limit_bytes=60 * 1024 * 1024
         ),
     )(
-        tokens, gain.reshape(1, -1), w_query, w_key, w_value, w_inner, bias.reshape(1, -1),
+        tokens, gain.reshape(1, -1), w_query, w_key, w_value, w_inner, bias,
         w_attn_out, w_outer, temper.reshape(1, 1),
     )
 

time: 87.4 us -> 81 us (0.927)
  Pallas kernels: 83.9 us -> 78.7 us
  local copies, waits for them, and re-layouts: 2.7 us -> 1.44 us
    pallas_call x1, Pallas kernels: 83.9 us -> 78.7 us  [per_device(): pl.pallas_call(kernel, out_shape=jax.ShapeDtypeStruct(tokens.shape, BF),...]
    reshape x1 -> x0, local copies, waits for them, and re-layouts: 1.27 us -> none  [per_device(): bias.reshape(1, -1)]
where the time goes in v2:
time: 81 us; the launch traced here: 80.8 us
  Pallas kernels  78.7 us (97%)
  local copies, waits for them, and re-layouts  1.44 us (2%)
    pallas_call x1, Pallas kernels, per_device(): pl.pallas_call(kernel, out_shape=jax.ShapeDtypeStruct(tokens.shape, BF),...  78.7 us

profile of v2, /device:TPU:1, one launch (start us, length us, event | category | flops | bytes accessed | tf_op | source)
XLA Modules:
  0.0 80.8 jit_solution(4413186007470174046)
XLA Ops:
  0.7 78.7 %shard_map.100 = bf16[4,6144]{1,0:T(4,128)(2,1)} custom-call(bf16[4,6144]{1,0:T(4,128)(2,1)} %tok_ref.1, f32[1,6144]{1,0:T(1,128)} %bitcast.3, bf16[768,128]{1,0:T(8,128)(2,1)} %wq_ref.1, bf16[768,128]{1,0:T(8,128)(2,1)} %wk_ref.1, bf16[768,128]{1,0:T(8,128)(2,1)} %wv_ref.1, bf16[768,768]{1,0:T(8,128)(2,1)} %wi_ref.1, f32[768]{0:T(1024)} %bias_ref.1, ...), custom_call_target="tpu_custom_call" | custom-call | tf_op jit(solution)/shard_map/pallas_call | solution.py:344
  79.4 1.4 %copy.13 = bf16[4,6144]{1,0:T(4,128)(2,1)} copy(bf16[4,6144]{1,0:T(4,128)(2,1)} %shard_map.100) | data formatting | bytes 98304
